TPU v7x, 16 devices: a whole 2x2x2 slice. The times are simulated.
16 devices in a mesh: data: 16 (over z, y, x, core).
Axes of the slice: x: 2, y: 2, z: 2, core: 2. Of those that a mesh axis runs over, the one named last changes fastest.
Arguments:
- x_in: bfloat16 [32768, 1024], P('data')
- dy_in: bfloat16 [32768, 1024], P('data')
- weights: bfloat16 [4, 1024, 1024], replicated
- a_old: float32 [4096, 1024], P('data')
- s_old: float32 [4096, 1024], P('data')
- a_inv: float32 [4096, 1024], P('data')
- s_inv: float32 [4, 1024, 1024], replicated
Outputs:
- output 1: float32 [4, 1024, 1024], replicated
- output 2: float32 [4096, 1024], P('data')
- output 3: float32 [4096, 1024], P('data')
All inputs are finite; a program needn't handle non-finite values.
Results may differ from a plain program's by a relative error of at most 0.00181429.
Values are sent between devices in bfloat16 or wider.
A program may use at most 1 GiB of HBM per device.

v0:
```python
import functools
import jax
import jax.numpy as jnp
from jax import lax
from jax.sharding import PartitionSpec as P

FACTOR_DECAY = 0.75
PRECISE = lax.Precision.HIGHEST


def gelu_grad(pre_act, d_act):
    pullback = jax.vjp(functools.partial(jax.nn.gelu, approximate=True), pre_act.astype(jnp.float32))[1]
    return pullback(d_act.astype(jnp.float32))[0].astype(jnp.bfloat16)


def cross_rows(left_op, right_op):
    return jnp.einsum("bi,bj->ij", left_op, right_op, preferred_element_type=jnp.float32)


def local_pass(x_loc, dy_loc, weights):
    n_layers = weights.shape[0]
    layer_inputs = [x_loc]
    pre_acts = []
    for layer_id in range(n_layers - 1):
        pre_act = jnp.dot(layer_inputs[layer_id], weights[layer_id], preferred_element_type=jnp.float32).astype(jnp.bfloat16)
        pre_acts.append(pre_act)
        layer_inputs.append(jax.nn.gelu(pre_act.astype(jnp.float32), approximate=True).astype(jnp.bfloat16))
    out_grads = [dy_loc] * n_layers
    for layer_id in range(n_layers - 1, 0, -1):
        d_act = jnp.einsum("bj,ij->bi", out_grads[layer_id], weights[layer_id], preferred_element_type=jnp.float32).astype(jnp.bfloat16)
        out_grads[layer_id - 1] = gelu_grad(pre_acts[layer_id - 1], d_act)
    return layer_inputs, out_grads


def solution(mesh):
    n_dev = mesh.shape["data"]

    def device_step(x_loc, dy_loc, weights, a_old_rows, s_old_rows, a_inv_rows, s_inv):
        n_layers = weights.shape[0]
        model_width = weights.shape[1]
        batch_total = x_loc.shape[0] * n_dev
        layer_inputs, out_grads = local_pass(x_loc, dy_loc, weights)
        a_loc = jnp.concatenate([cross_rows(h_in, h_in) for h_in in layer_inputs], axis=0) / batch_total
        s_loc = jnp.concatenate([cross_rows(g_out, g_out) for g_out in out_grads], axis=0) / batch_total
        w_loc = jnp.stack([cross_rows(h_in, g_out) for h_in, g_out in zip(layer_inputs, out_grads)]) / batch_total
        a_sum = lax.psum_scatter(a_loc, "data", scatter_dimension=0, tiled=True)
        s_sum = lax.psum_scatter(s_loc, "data", scatter_dimension=0, tiled=True)
        w_grad = lax.psum(w_loc, "data")
        own_rows = a_old_rows.shape[0]
        layer_id = (lax.axis_index("data") * own_rows) // model_width
        w_grad_own = lax.dynamic_index_in_dim(w_grad, layer_id, axis=0, keepdims=False)
        s_inv_own = lax.dynamic_index_in_dim(s_inv, layer_id, axis=0, keepdims=False)
        left_prod = jnp.dot(a_inv_rows, w_grad_own, precision=PRECISE)
        u_rows = jnp.dot(left_prod, s_inv_own, precision=PRECISE)
        u_full = lax.all_gather(u_rows, "data", axis=0, tiled=True).reshape(n_layers, model_width, model_width)
        a_new = FACTOR_DECAY * a_old_rows + (1.0 - FACTOR_DECAY) * a_sum
        s_new = FACTOR_DECAY * s_old_rows + (1.0 - FACTOR_DECAY) * s_sum
        return u_full, a_new, s_new

    row_spec = P("data", None)
    return jax.shard_map(
        device_step,
        mesh=mesh,
        in_specs=(row_spec, row_spec, P(), row_spec, row_spec, row_spec, P()),
        out_specs=(P(), row_spec, row_spec),
        check_vma=False,
    )
```

profile of v0, /device:TPU:0, one launch (start us, length us, event | category | flops | bytes accessed | tf_op | source)
XLA Modules:
  0.0 721.5 jit_solution(13686808662698069275)
XLA Ops:
  7.2 0.0 copy-start
  7.2 0.0 all-reduce.2.cloned.1.call-start
  7.2 7.5 %convolution_convert_fusion.2 = bf16[2048,1024]{1,0:T(8,128)(2,1)S(1)} fusion(bf16[2048,1024]{1,0:T(8,128)(2,1)} %param.7, bf16[4,1024,1024]{2,1,0:T(8,128)(2,1)} %param.9), kind=kOutput, calls=%fused_computation.62 | convolution fusion | flops 4297064448 | bytes 10485760 | tf_op jit(solution)/shard_map/dot_general | solution.py:25
  14.8 6.1 convolution_convert_fusion.1
  20.9 0.0 copy-start.17
  20.9 0.0 copy-start.5
  20.9 5.6 convolution_convert_fusion
  26.6 1.9 copy-done.14
  28.5 9.6 %fusion.5 = bf16[2048,1024]{1,0:T(8,128)(2,1)S(1)} fusion(bf16[2048,1024]{1,0:T(8,128)(2,1)S(1)} %convolution_convert_fusion, bf16[2048,1024]{1,0:T(8,128)(2,1)S(1)} %copy-done.5, bf16[4,1024,1024]{2,1,0:T(8,128)(2,1)S(1)} %copy-done.3), kind=kOutput, calls=%fused_computation.26 | convolution fusion | flops 4343201792 | bytes 14680064 | tf_op jit(solution)/shard_map/bj,ij->bi/dot_general | solution.py:30
  38.1 0.0 copy-done.17
  38.1 0.0 copy-start.7
  38.1 9.6 %fusion.8 = bf16[2048,1024]{1,0:T(8,128)(2,1)S(1)} fusion(bf16[2048,1024]{1,0:T(8,128)(2,1)S(1)} %convolution_convert_fusion.1, bf16[2048,1024]{1,0:T(8,128)(2,1)S(1)} %fusion.5, bf16[4,1024,1024]{2,1,0:T(8,128)(2,1)S(1)} %copy-done.3), kind=kOutput, calls=%fused_computation.29 | convolution fusion | flops 4343201792 | bytes 14680064 | tf_op jit(solution)/shard_map/bj,ij->bi/dot_general | solution.py:30
  47.8 9.8 %fusion.11 = bf16[2048,1024]{1,0:T(8,128)(2,1)S(1)} fusion(bf16[2048,1024]{1,0:T(8,128)(2,1)S(1)} %convolution_convert_fusion.2, bf16[2048,1024]{1,0:T(8,128)(2,1)S(1)} %fusion.8, bf16[4,1024,1024]{2,1,0:T(8,128)(2,1)S(1)} %copy-done.3), kind=kOutput, calls=%fused_computation.32 | convolution fusion | flops 4343201792 | bytes 14680064 | tf_op jit(solution)/shard_map/bj,ij->bi/dot_general | solution.py:30
  57.7 5.1 convolution_bitcast_fusion.2
  62.7 7.1 convolution_bitcast_fusion.1
  69.8 0.0 copy-start.4
  69.8 5.1 convolution_bitcast_fusion
  74.9 4.7 convolution_bitcast_fusion.3
  79.7 6.4 maximum_multiply_fusion
  86.0 0.0 all-reduce.2.cloned.1.call-update
  86.1 0.0 reduce-scatter.3.cloned.1.call-start
  86.1 8.1 %fusion.64 = f32[1024,1024]{1,0:T(8,128)S(1)} fusion(bf16[2048,1024]{1,0:T(8,128)(2,1)} %param.7), kind=kOutput, calls=%fused_computation.86 | convolution fusion | flops 4294967296 | bytes 8388608 | tf_op jit(solution)/shard_map/bi,bj->ij/dot_general | solution.py:17
  94.3 7.8 %fusion.60 = f32[1024,1024]{1,0:T(8,128)S(1)} fusion(bf16[2048,1024]{1,0:T(8,128)(2,1)S(1)} %copy-done.13), kind=kOutput, calls=%fused_computation.85 | convolution fusion | flops 4315938816 | bytes 8388608 | tf_op jit(solution)/shard_map/bi,bj->ij/dot_general | solution.py:17
  102.1 7.8 %fusion.56 = f32[1024,1024]{1,0:T(8,128)S(1)} fusion(bf16[2048,1024]{1,0:T(8,128)(2,1)S(1)} %copy-done.18), kind=kOutput, calls=%fused_computation.84 | convolution fusion | flops 4315938816 | bytes 8388608 | tf_op jit(solution)/shard_map/bi,bj->ij/dot_general | solution.py:17
  109.9 7.8 %fusion.53 = f32[1024,1024]{1,0:T(8,128)S(1)} fusion(bf16[2048,1024]{1,0:T(8,128)(2,1)S(1)} %copy-done.16), kind=kOutput, calls=%fused_computation.83 | convolution fusion | flops 4315938816 | bytes 8388608 | tf_op jit(solution)/shard_map/bi,bj->ij/dot_general | solution.py:17
  117.7 7.3 %maximum_multiply_fusion.1 = f32[4096,1024]{1,0:T(8,128)} fusion(f32[1024,1024]{1,0:T(8,128)S(1)} %fusion.53, f32[1024,1024]{1,0:T(8,128)S(1)} %fusion.56, f32[1024,1024]{1,0:T(8,128)S(1)} %fusion.60, f32[1024,1024]{1,0:T(8,128)S(1)} %fusion.64), kind=kLoop, calls=%fused_computation.1 | loop fusion | flops 16777216 | bytes 33554432 | tf_op jit(solution)/shard_map/div | solution.py:43
  125.0 0.0 reduce-scatter.3.cloned.1.call-update
  125.0 0.0 reduce-scatter.5.cloned.1.call-start
  125.0 7.9 %fusion.65 = f32[1024,1024]{1,0:T(8,128)S(1)} fusion(bf16[2048,1024]{1,0:T(8,128)(2,1)} %copy-done.11), kind=kOutput, calls=%fused_computation.87 | convolution fusion | flops 4294967296 | bytes 8388608 | tf_op jit(solution)/shard_map/bi,bj->ij/dot_general | solution.py:17
  133.0 4.7 fusion.66
  137.8 0.0 copy-start.6
  137.8 4.7 fusion.67
  142.5 5.0 fusion.68
  147.5 7.3 %maximum_multiply_fusion.2 = f32[4096,1024]{1,0:T(8,128)} fusion(f32[1024,1024]{1,0:T(8,128)S(1)} %fusion.68, f32[1024,1024]{1,0:T(8,128)S(1)} %fusion.67, f32[1024,1024]{1,0:T(8,128)S(1)} %fusion.66, f32[1024,1024]{1,0:T(8,128)S(1)} %fusion.65), kind=kLoop, calls=%fused_computation.2 | loop fusion | flops 16777216 | bytes 33554432 | tf_op jit(solution)/shard_map/div | solution.py:44
  154.8 0.0 reduce-scatter.5.cloned.1.call-update
  154.8 0.0 copy-start.1
  154.8 0.0 all-gather.2.cloned.1.call-start
  154.9 0.0 copy-start.2
  154.9 113.9 %all-reduce.2.cloned.1.call-done = f32[4,1024,1024]{1,2,0:T(8,128)} async-done(((f32[4,1024,1024]{1,2,0:T(8,128)}), f32[4,1024,1024]{1,2,0:T(8,128)}) %all-reduce.2.cloned.1.call-update) | async-done | bytes 16777232 | tf_op jit(solution)/shard_map/psum | solution.py:48
  268.9 5.3 fusion.35
  274.2 6.9 fusion.33
  281.0 0.0 all-gather.2.cloned.1.call-update
  281.1 166.9 %reduce-scatter.3.cloned.1.call-done = f32[256,1024]{1,0:T(8,128)} async-done(((f32[4096,1024]{1,0:T(8,128)}), f32[256,1024]{1,0:T(8,128)}) %reduce-scatter.3.cloned.1.call-update) | async-done | bytes 1048592 | tf_op jit(solution)/shard_map/reduce_scatter | solution.py:46
  447.9 2.4 multiply_add_fusion.1
  450.3 175.5 %reduce-scatter.5.cloned.1.call-done = f32[256,1024]{1,0:T(8,128)} async-done(((f32[4096,1024]{1,0:T(8,128)}), f32[256,1024]{1,0:T(8,128)}) %reduce-scatter.5.cloned.1.call-update) | async-done | bytes 1048592 | tf_op jit(solution)/shard_map/reduce_scatter | solution.py:47
  625.7 2.4 multiply_add_fusion
  628.1 74.6 %all-gather.2.cloned.1.call-done = f32[4096,1024]{1,0:T(8,128)} async-done(((f32[256,1024]{1,0:T(8,128)}), f32[4096,1024]{1,0:T(8,128)}) %all-gather.2.cloned.1.call-update) | async-done | bytes 16777232 | tf_op jit(solution)/shard_map/all_gather | solution.py:55
  702.7 12.0 %copy.18 = f32[4,1024,1024]{2,1,0:T(8,128)} copy(f32[4,1024,1024]{2,1,0:T(8,128)} %bitcast.54) | data formatting | bytes 33554432
  (28 shorter events, 0.1 us)
Async XLA Ops:
  7.2 261.7 %copy-start = (f32[256,1024]{1,0:T(8,128)S(1)}, f32[256,1024]{1,0:T(8,128)}, u32[]{:S(2)}) copy-start(f32[256,1024]{1,0:T(8,128)} %param.12) | copy-start | bytes 3145732
  7.2 261.7 %all-reduce.2.cloned.1.call-start = ((), (), s32[]{:S(2)}) async-start(), calls=%async_computation.2 | async-start | bytes 33554432 | tf_op jit(solution)/shard_map/psum | solution.py:48
  7.2 7.6 %copy-start.3 = (bf16[4,1024,1024]{2,1,0:T(8,128)(2,1)S(1)}, bf16[4,1024,1024]{2,1,0:T(8,128)(2,1)}, u32[]{:S(2)}) copy-start(bf16[4,1024,1024]{2,1,0:T(8,128)(2,1)} %param.9) | copy-start | bytes 25165828
  14.8 42.8 %copy-start.12 = (bf16[2048,1024]{1,0:T(8,128)(2,1)}, bf16[2048,1024]{1,0:T(8,128)(2,1)S(1)}, u32[]{:S(2)}) copy-start(bf16[2048,1024]{1,0:T(8,128)(2,1)S(1)} %convolution_convert_fusion.2) | copy-start | bytes 12582916
  20.9 17.2 %copy-start.17 = (bf16[2048,1024]{1,0:T(8,128)(2,1)}, bf16[2048,1024]{1,0:T(8,128)(2,1)S(1)}, u32[]{:S(2)}) copy-start(bf16[2048,1024]{1,0:T(8,128)(2,1)S(1)} %convolution_convert_fusion.1) | copy-start | bytes 12582916
  20.9 7.6 %copy-start.5 = (bf16[2048,1024]{1,0:T(8,128)(2,1)S(1)}, bf16[2048,1024]{1,0:T(8,128)(2,1)}, u32[]{:S(2)}) copy-start(bf16[2048,1024]{1,0:T(8,128)(2,1)} %param.8) | copy-start | bytes 12582916
  26.6 1.9 copy-start.14
  38.1 24.6 %copy-start.7 = (bf16[2048,1024]{1,0:T(8,128)(2,1)}, bf16[2048,1024]{1,0:T(8,128)(2,1)S(1)}, u32[]{:S(2)}) copy-start(bf16[2048,1024]{1,0:T(8,128)(2,1)S(1)} %fusion.5) | copy-start | bytes 12582916
  47.8 9.8 %copy-start.9 = (bf16[2048,1024]{1,0:T(8,128)(2,1)}, bf16[2048,1024]{1,0:T(8,128)(2,1)S(1)}, u32[]{:S(2)}) copy-start(bf16[2048,1024]{1,0:T(8,128)(2,1)S(1)} %fusion.8) | copy-start | bytes 12582916
  57.6 17.2 %copy-start.11 = (bf16[2048,1024]{1,0:T(8,128)(2,1)}, bf16[2048,1024]{1,0:T(8,128)(2,1)S(1)}, u32[]{:S(2)}) copy-start(bf16[2048,1024]{1,0:T(8,128)(2,1)S(1)} %fusion.11) | copy-start | bytes 12582916
  62.7 7.1 copy-start.15
  69.8 5.1 copy-start.4
  86.1 361.9 %reduce-scatter.3.cloned.1.call-start = ((), (), s32[]{:S(2)}) async-start(), calls=%async_computation.4 | async-start | bytes 17825792 | tf_op jit(solution)/shard_map/reduce_scatter | solution.py:46
  86.1 8.2 %copy-start.13 = (bf16[2048,1024]{1,0:T(8,128)(2,1)S(1)}, bf16[2048,1024]{1,0:T(8,128)(2,1)}, u32[]{:S(2)}) copy-start(bf16[2048,1024]{1,0:T(8,128)(2,1)} %copy-done.12) | copy-start | bytes 12582916
  94.3 7.8 %copy-start.18 = (bf16[2048,1024]{1,0:T(8,128)(2,1)S(1)}, bf16[2048,1024]{1,0:T(8,128)(2,1)}, u32[]{:S(2)}) copy-start(bf16[2048,1024]{1,0:T(8,128)(2,1)} %copy-done.17) | copy-start | bytes 12582916
  102.1 7.8 %copy-start.16 = (bf16[2048,1024]{1,0:T(8,128)(2,1)S(1)}, bf16[2048,1024]{1,0:T(8,128)(2,1)}, u32[]{:S(2)}) copy-start(bf16[2048,1024]{1,0:T(8,128)(2,1)} %copy-done.14) | copy-start | bytes 12582916
  125.0 500.8 %reduce-scatter.5.cloned.1.call-start = ((), (), s32[]{:S(2)}) async-start(), calls=%async_computation.5 | async-start | bytes 17825792 | tf_op jit(solution)/shard_map/reduce_scatter | solution.py:47
  125.0 8.0 %copy-start.10 = (bf16[2048,1024]{1,0:T(8,128)(2,1)S(1)}, bf16[2048,1024]{1,0:T(8,128)(2,1)}, u32[]{:S(2)}) copy-start(bf16[2048,1024]{1,0:T(8,128)(2,1)} %copy-done.9) | copy-start | bytes 12582916
  133.0 4.7 copy-start.8
  137.8 4.7 copy-start.6
  154.8 293.1 %copy-start.1 = (f32[256,1024]{1,0:T(8,128)S(1)}, f32[256,1024]{1,0:T(8,128)}, u32[]{:S(2)}) copy-start(f32[256,1024]{1,0:T(8,128)} %param.10) | copy-start | bytes 3145732
  154.8 547.9 %all-gather.2.cloned.1.call-start = ((), (), s32[]{:S(2)}) async-start(), calls=%async_computation.3 | async-start | bytes 17825792 | tf_op jit(solution)/shard_map/all_gather | solution.py:55
  154.9 470.8 %copy-start.2 = (f32[256,1024]{1,0:T(8,128)S(1)}, f32[256,1024]{1,0:T(8,128)}, u32[]{:S(2)}) copy-start(f32[256,1024]{1,0:T(8,128)} %param.11) | copy-start | bytes 3145732
Sparse Core Ops, SparseCore 0:
  86.2 182.6 all-reduce.1
  271.1 176.7 reduce-scatter.2
  450.2 175.4 reduce-scatter.4
  628.4 74.2 all-gather.1
where the time goes:
time: 725 us; the launch traced here: 721 us
  waiting for transfers between devices  531 us (73%)
  matrix products  136 us (19%)
  other arithmetic  25.7 us (4%)
  between operations  14.5 us (2%)
  local copies, waits for them, and re-layouts  14 us (2%)
    reduce_scatter x1, waiting for transfers between devices, device_step(): s_sum = lax.psum_scatter(s_loc, 'data', scatter_dimension=0, tiled=True)  175 us
    reduce_scatter x1, waiting for transfers between devices, device_step(): a_sum = lax.psum_scatter(a_loc, 'data', scatter_dimension=0, tiled=True)  167 us
    psum x1, waiting for transfers between devices, device_step(): w_grad = lax.psum(w_loc, 'data')  114 us
    dot_general x12, matrix products, cross_rows(): jnp.einsum('bi,bj->ij', left_op, right_op, preferred_element_type=jnp.flo...  75.7 us
    all_gather x1, waiting for transfers between devices, device_step(): lax.all_gather(u_rows, 'data', axis=0, tiled=True)  74.6 us
    dot_general x3, matrix products, local_pass(): jnp.einsum('bj,ij->bi', out_grads[layer_id], weights[layer_id], preferred...  29.1 us
    dot_general x3, matrix products, local_pass(): jnp.dot(layer_inputs[layer_id], weights[layer_id], preferred_element_type...  19.3 us
  transfers between devices with their start and end apart: 4, of which 4 were waited for; matrix products, arithmetic and copies ran while one was open for 12% of the time, Pallas kernels for 0%

commit v1 on v0

v1 whole, which is shorter than its diff:
```python
import functools
import jax
import jax.numpy as jnp
from jax import lax
from jax.experimental import pallas as pl
from jax.experimental.pallas import tpu as pltpu
from jax.sharding import PartitionSpec as P

FACTOR_DECAY = 0.75
PRECISE = lax.Precision.HIGHEST
MESH = pl.DeviceIdType.MESH
PAD = 16
CORE, X, Y, Z = 1, 2, 4, 8
PARTS = ((0, 384, (X, Y, Z)), (384, 384, (Y, Z, X)), (768, 256, (Z, X, Y)))


def gelu_grad(pre_act, d_act):
    pullback = jax.vjp(functools.partial(jax.nn.gelu, approximate=True), pre_act.astype(jnp.float32))[1]
    return pullback(d_act.astype(jnp.float32))[0].astype(jnp.bfloat16)


def cross_rows(left_op, right_op):
    return jnp.einsum("bi,bj->ij", left_op, right_op, preferred_element_type=jnp.float32)


def encode(value, top):
    w = value * (131072.0 / top)
    w2 = w * w
    return (w * w2 * (w2 * w2)).astype(jnp.bfloat16)


def decode(code, top):
    y = code.astype(jnp.float32)
    mag = jnp.abs(y)
    root = jnp.exp(jnp.log(jnp.where(mag > 0.0, mag, 1.0)) * (1.0 / 7.0)) * (top * (1.0 / 131072.0))
    return jnp.where(y > 0.0, root, jnp.where(y < 0.0, -root, 0.0))


def block_top(value):
    top = jnp.maximum(jnp.max(jnp.abs(value)), 1e-30) * 1.01
    return top.astype(jnp.bfloat16).astype(jnp.float32)


def tail_kernel(g_ref, ainv_ref, sinv_hbm, u_ref, sinv, t_all, t_out, t_in, own_sem, t_send, t_recv, u_send, u_recv):
    rows = g_ref.shape[0]
    width = g_ref.shape[1]
    me = lax.axis_index("data")
    core = lax.rem(me, 2)
    xx = lax.rem(me // 2, 2)
    yy = lax.rem(me // 4, 2)
    zz = me // 8
    off = {CORE: 1 - 2 * core, X: 2 * (1 - 2 * xx), Y: 4 * (1 - 2 * yy), Z: 8 * (1 - 2 * zz)}

    load = pltpu.make_async_copy(sinv_hbm.at[me // 4], sinv, own_sem)
    load.start()
    barrier = pltpu.get_barrier_semaphore()
    for d in (CORE, X, Y, Z):
        pl.semaphore_signal(barrier, inc=1, device_id=(me + off[d],), device_id_type=MESH)
    pl.semaphore_wait(barrier, 4)
    load.wait()

    own = 2 * xx + core
    chunk = 256

    @pl.loop(0, width // chunk)
    def _(j):
        cols = pl.ds(pl.multiple_of(j * chunk, chunk), chunk)
        t_all[own, :, cols] = jnp.dot(g_ref[...], sinv[:, cols], precision=PRECISE)

    t_top = block_top(t_all[own])
    t_out[pl.ds(0, rows), :] = encode(t_all[own], t_top)
    t_out[pl.ds(rows, PAD), :] = jnp.full((PAD, width), t_top, jnp.bfloat16)

    def send(src, dst, d, sems, i):
        copy = pltpu.make_async_remote_copy(
            src_ref=src, dst_ref=dst, send_sem=sems[0].at[i], recv_sem=sems[1].at[i],
            device_id=(me + off[d],), device_id_type=MESH)
        copy.start()
        return copy

    t_sems = (t_send, t_recv)
    across = send(t_out, t_in.at[0], X, t_sems, 0)
    beside = send(t_out, t_in.at[1], CORE, t_sems, 1)
    across.wait_recv()
    diag = send(t_in.at[0], t_in.at[2], CORE, t_sems, 2)
    beside.wait_recv()
    diag.wait_recv()

    def take(code_ref):
        return decode(code_ref[pl.ds(0, rows), :], code_ref[pl.ds(rows, 1), pl.ds(0, 1)].astype(jnp.float32))

    t_all[2 * (1 - xx) + core] = take(t_in.at[0])
    t_all[2 * xx + 1 - core] = take(t_in.at[1])
    t_all[2 * (1 - xx) + 1 - core] = take(t_in.at[2])

    u_rows = sinv

    @pl.loop(0, width // chunk)
    def _(j):
        cols = pl.ds(pl.multiple_of(j * chunk, chunk), chunk)
        acc = jnp.zeros((rows, chunk), jnp.float32)
        for k in range(4):
            acc += jnp.dot(ainv_ref[:, k * rows:(k + 1) * rows], t_all[k, :, cols], precision=PRECISE)
        u_rows[pl.ds(0, rows), cols] = acc

    u_top = block_top(u_rows[pl.ds(0, rows), :])
    u_ref[me, pl.ds(0, rows), :] = encode(u_rows[pl.ds(0, rows), :], u_top)
    u_ref[me, pl.ds(rows, PAD), :] = jnp.full((PAD, width), u_top, jnp.bfloat16)
    across.wait_send()
    beside.wait_send()
    diag.wait_send()

    u_sems = (u_send, u_recv)
    sent = []

    def pass_on(slot, part, d, i):
        first, size, _ = PARTS[part]
        ref = u_ref.at[slot, :, pl.ds(first, size)]
        copy = send(ref, ref, d, u_sems, part * 15 + i)
        sent.append(copy)
        return copy

    slots = [[me] for _ in PARTS]
    waits = [[] for _ in PARTS]
    core_i = [7 for _ in PARTS]
    last = []
    for stage in range(3):
        for part, (_, _, order) in enumerate(PARTS):
            for copy in waits[part]:
                copy.wait_recv()
            d = order[stage]
            base = (1 << stage) - 1
            waits[part] = [pass_on(s, part, d, base + k) for k, s in enumerate(slots[part])]
            fresh = slots[part] if stage == 0 else slots[part][len(slots[part]) // 2:]
            for s in fresh:
                last.append(pass_on(s, part, CORE, core_i[part]))
                core_i[part] += 1
            slots[part] = slots[part] + [s + off[d] for s in slots[part]]
    for part in range(len(PARTS)):
        for copy in waits[part]:
            copy.wait_recv()
        for s in slots[part][4:]:
            last.append(pass_on(s, part, CORE, core_i[part]))
            core_i[part] += 1
    for copy in last:
        copy.wait_recv()
    for copy in sent:
        copy.wait_send()


def tail(g_rows, a_inv_rows, s_inv, n_dev):
    rows, width = g_rows.shape
    block = (rows + PAD, width)
    vmem = pl.BlockSpec(memory_space=pltpu.VMEM)
    return pl.pallas_call(
        tail_kernel,
        out_shape=jax.ShapeDtypeStruct((n_dev,) + block, jnp.bfloat16),
        in_specs=[vmem, vmem, pl.BlockSpec(memory_space=pl.ANY)],
        out_specs=vmem,
        scratch_shapes=[
            pltpu.VMEM((width, width), jnp.float32),
            pltpu.VMEM((4, rows, width), jnp.float32),
            pltpu.VMEM(block, jnp.bfloat16),
            pltpu.VMEM((3,) + block, jnp.bfloat16),
            pltpu.SemaphoreType.DMA,
            pltpu.SemaphoreType.DMA((3,)),
            pltpu.SemaphoreType.DMA((3,)),
            pltpu.SemaphoreType.DMA((45,)),
            pltpu.SemaphoreType.DMA((45,)),
        ],
        compiler_params=pltpu.CompilerParams(collective_id=0, has_side_effects=True, vmem_limit_bytes=48 * 2**20),
        cost_estimate=pl.CostEstimate(flops=6 * 4 * rows * width * width, bytes_accessed=20 * 2**20, transcendentals=0),
    )(g_rows, a_inv_rows, s_inv)


def solution(mesh):
    n_dev = mesh.shape["data"]

    def device_step(x_loc, dy_loc, weights, a_old_rows, s_old_rows, a_inv_rows, s_inv):
        n_layers, width = weights.shape[0], weights.shape[1]
        rows = a_old_rows.shape[0]
        batch_total = x_loc.shape[0] * n_dev
        me = lax.axis_index("data")
        bit = {CORE: me % 2, X: (me // 2) % 2, Y: (me // 4) % 2, Z: me // 8}

        def swap(value, d, wire):
            out = lax.ppermute(value.astype(wire), "data", [(p, p ^ d) for p in range(n_dev)])
            return out.astype(jnp.float32)

        def gather_pair(full, wires):
            blocks = full.reshape(2, 2, rows, width)
            theirs = lax.dynamic_index_in_dim(blocks, 1 - bit[CORE], 1, keepdims=False)
            mine = lax.dynamic_index_in_dim(blocks, bit[CORE], 1, keepdims=False)
            got = swap(theirs, CORE, jnp.float32)

            def pick(i):
                return lax.dynamic_index_in_dim(mine, i, 0, keepdims=False) + lax.dynamic_index_in_dim(got, i, 0, keepdims=False)

            return pick(bit[X]) + swap(pick(1 - bit[X]), X, wires[0])

        def gather_plane(layers, wires):
            half = width // 2
            pieces = []
            for first, (d1, d2) in ((0, (Z, Y)), (half, (Y, Z))):
                part = [v[:, first:first + half] for v in layers]
                if d1 == Z:
                    pairs = [(part[0], part[2]), (part[1], part[3])]
                else:
                    pairs = [(part[0], part[1]), (part[2], part[3])]
                low = bit[d1] == 0
                send = jnp.stack([jnp.where(low, hi, lo) for lo, hi in pairs])
                keep = jnp.stack([jnp.where(low, lo, hi) for lo, hi in pairs])
                both = keep + swap(send, d1, wires[1])
                low = bit[d2] == 0
                out = jnp.where(low, both[0], both[1]) + swap(jnp.where(low, both[1], both[0]), d2, wires[2])
                pieces.append(out)
            return jnp.concatenate(pieces, axis=1)

        a_wires = (jnp.bfloat16, jnp.bfloat16, jnp.float32)
        g_wires = (jnp.bfloat16, jnp.float32, jnp.float32)

        layer_inputs, pre_acts, a_parts = [x_loc], [], []
        for layer_id in range(n_layers - 1):
            pre_act = jnp.dot(layer_inputs[layer_id], weights[layer_id], preferred_element_type=jnp.float32).astype(jnp.bfloat16)
            pre_acts.append(pre_act)
            layer_inputs.append(jax.nn.gelu(pre_act.astype(jnp.float32), approximate=True).astype(jnp.bfloat16))
        out_grads = [dy_loc] * n_layers
        for layer_id in range(n_layers - 1, 0, -1):
            d_act = jnp.einsum("bj,ij->bi", out_grads[layer_id], weights[layer_id], preferred_element_type=jnp.float32).astype(jnp.bfloat16)
            out_grads[layer_id - 1] = gelu_grad(pre_acts[layer_id - 1], d_act)

        a_parts = [gather_pair(cross_rows(h_in, h_in), a_wires) for h_in in layer_inputs]
        w_parts = [gather_pair(cross_rows(h_in, g_out), g_wires) for h_in, g_out in zip(layer_inputs, out_grads)]
        w_own = gather_plane(w_parts, g_wires)
        s_parts = [gather_pair(cross_rows(g_out, g_out), a_wires) for g_out in out_grads]
        a_own = gather_plane(a_parts, a_wires)
        s_own = gather_plane(s_parts, a_wires)

        u_code = tail(w_own * (1.0 / batch_total), a_inv_rows, s_inv, n_dev)
        u_full = decode(u_code[:, :rows], u_code[:, rows:rows + 1, :1].astype(jnp.float32)).reshape(n_layers, width, width)
        grow = (1.0 - FACTOR_DECAY) / batch_total
        a_new = FACTOR_DECAY * a_old_rows + grow * a_own
        s_new = FACTOR_DECAY * s_old_rows + grow * s_own
        return u_full, a_new, s_new

    row_spec = P("data", None)
    return jax.shard_map(
        device_step,
        mesh=mesh,
        in_specs=(row_spec, row_spec, P(), row_spec, row_spec, row_spec, P()),
        out_specs=(P(), row_spec, row_spec),
        check_vma=False,
    )
```

time: 725 us -> 494 us (0.68)
  waiting for transfers between devices: 531 us -> 138 us
  Pallas kernels: 0 us -> 72.1 us
  other arithmetic: 25.7 us -> 65.9 us
  starting transfers between devices: 0.16 us -> 38.3 us
  local copies, waits for them, and re-layouts: 14 us -> 36.6 us
  between operations: 14.5 us -> 1.9 us
    reduce_scatter x2 -> x0, waiting for transfers between devices: 342 us -> none  [the longest x1 175 us: device_step(): s_sum = lax.psum_scatter(s_loc, 'data', scatter_dimension=0, tiled=True)]
    ppermute x0 -> x36, waiting for transfers between devices: none -> 138 us  [swap(): lax.ppermute(value.astype(wire), 'data', [(p, p ^ d) for p in range(n_dev)])]
    psum x1 -> x0, waiting for transfers between devices: 114 us -> none  [device_step(): w_grad = lax.psum(w_loc, 'data')]
    all_gather x1 -> x0, waiting for transfers between devices: 74.6 us -> none  [device_step(): lax.all_gather(u_rows, 'data', axis=0, tiled=True)]
    pallas_call x0 -> x1, Pallas kernels: none -> 72.1 us  [tail(): pl.pallas_call(tail_kernel, out_shape=jax.ShapeDtypeStruct((n_dev,) + blo...]
    ppermute x0 -> x36, starting transfers between devices: none -> 38.3 us  [swap(): lax.ppermute(value.astype(wire), 'data', [(p, p ^ d) for p in range(n_dev)])]
    convert_element_type x0 -> x12, other arithmetic: none -> 24.3 us  [swap(): value.astype(wire)]
    squeeze x0 -> x12, local copies, waits for them, and re-layouts: none -> 22 us  [gather_pair(): theirs = lax.dynamic_index_in_dim(blocks, 1 - bit[CORE], 1, keepdims=False)]
  transfers between devices with their start and end apart: 4 -> 36, of which waited for: 4 -> 13; matrix products, arithmetic and copies ran while one was open for 12% -> 31% of each run, Pallas kernels for 0% -> 0%
where the time goes in v1:
time: 494 us; the launch traced here: 490 us
  waiting for transfers between devices  138 us (28%)
  matrix products  137 us (28%)
  Pallas kernels  72.1 us (15%)
  other arithmetic  65.9 us (13%)
  starting transfers between devices  38.3 us (8%)
  local copies, waits for them, and re-layouts  36.6 us (7%)
    ppermute x36, waiting for transfers between devices, swap(): lax.ppermute(value.astype(wire), 'data', [(p, p ^ d) for p in range(n_dev)])  138 us
    dot_general x12, matrix products, cross_rows(): jnp.einsum('bi,bj->ij', left_op, right_op, preferred_element_type=jnp.flo...  88.8 us
    pallas_call x1, Pallas kernels, tail(): pl.pallas_call(tail_kernel, out_shape=jax.ShapeDtypeStruct((n_dev,) + blo...  72.1 us
    ppermute x36, starting transfers between devices, swap(): lax.ppermute(value.astype(wire), 'data', [(p, p ^ d) for p in range(n_dev)])  38.3 us
    dot_general x3, matrix products, device_step(): jnp.einsum('bj,ij->bi', out_grads[layer_id], weights[layer_id], preferred...  28.9 us
    convert_element_type x12, other arithmetic, swap(): value.astype(wire)  24.3 us
    squeeze x12, local copies, waits for them, and re-layouts, gather_pair(): theirs = lax.dynamic_index_in_dim(blocks, 1 - bit[CORE], 1, keepdims=False)  22 us
    dot_general x3, matrix products, device_step(): jnp.dot(layer_inputs[layer_id], weights[layer_id], preferred_element_type...  18.9 us
  transfers between devices with their start and end apart: 36, of which 13 were waited for; matrix products, arithmetic and copies ran while one was open for 31% of the time, Pallas kernels for 0%

profile of v1, /device:TPU:0, one launch (start us, length us, event | category | flops | bytes accessed | tf_op | source)
XLA Modules:
  0.0 489.7 jit_solution(4828991763189912501)
XLA Ops:
  0.7 7.5 %convolution_convert_fusion.2 = bf16[2048,1024]{1,0:T(8,128)(2,1)S(1)} fusion(bf16[2048,1024]{1,0:T(8,128)(2,1)} %param.7, bf16[4,1024,1024]{2,1,0:T(8,128)(2,1)} %param.9), kind=kOutput, calls=%fused_computation.62 | convolution fusion | flops 4297064448 | bytes 10485760 | tf_op jit(solution)/shard_map/dot_general | solution.py:224
  8.2 5.8 %convolution_convert_fusion.1 = bf16[2048,1024]{1,0:T(8,128)(2,1)S(1)} fusion(bf16[4,1024,1024]{2,1,0:T(8,128)(2,1)S(1)} %copy-done.34, bf16[2048,1024]{1,0:T(8,128)(2,1)S(1)} %convolution_convert_fusion.2), kind=kOutput, calls=%fused_computation.61 | convolution fusion | flops 4318035968 | bytes 10485760 | tf_op jit(solution)/shard_map/dot_general | solution.py:224
  14.0 5.6 %convolution_convert_fusion = bf16[2048,1024]{1,0:T(8,128)(2,1)S(1)} fusion(bf16[4,1024,1024]{2,1,0:T(8,128)(2,1)S(1)} %copy-done.34, bf16[2048,1024]{1,0:T(8,128)(2,1)S(1)} %convolution_convert_fusion.1), kind=kOutput, calls=%fused_computation.60 | convolution fusion | flops 4318035968 | bytes 10485760 | tf_op jit(solution)/shard_map/dot_general | solution.py:224
  19.6 9.6 %fusion.9 = bf16[2048,1024]{1,0:T(8,128)(2,1)S(1)} fusion(bf16[2048,1024]{1,0:T(8,128)(2,1)S(1)} %convolution_convert_fusion, bf16[2048,1024]{1,0:T(8,128)(2,1)S(1)} %copy-done.36, bf16[4,1024,1024]{2,1,0:T(8,128)(2,1)S(1)} %copy-done.34), kind=kOutput, calls=%fused_computation.32 | convolution fusion | flops 4343201792 | bytes 14680064 | tf_op jit(solution)/shard_map/bj,ij->bi/dot_general | solution.py:229
  29.3 9.6 %fusion.12 = bf16[2048,1024]{1,0:T(8,128)(2,1)S(1)} fusion(bf16[2048,1024]{1,0:T(8,128)(2,1)S(1)} %convolution_convert_fusion.1, bf16[2048,1024]{1,0:T(8,128)(2,1)S(1)} %fusion.9, bf16[4,1024,1024]{2,1,0:T(8,128)(2,1)S(1)} %copy-done.34), kind=kOutput, calls=%fused_computation.35 | convolution fusion | flops 4343201792 | bytes 14680064 | tf_op jit(solution)/shard_map/bj,ij->bi/dot_general | solution.py:229
  39.0 9.6 %fusion.15 = bf16[2048,1024]{1,0:T(8,128)(2,1)S(1)} fusion(bf16[2048,1024]{1,0:T(8,128)(2,1)S(1)} %convolution_convert_fusion.2, bf16[2048,1024]{1,0:T(8,128)(2,1)S(1)} %fusion.12, bf16[4,1024,1024]{2,1,0:T(8,128)(2,1)S(1)} %copy-done.34), kind=kOutput, calls=%fused_computation.38 | convolution fusion | flops 4343201792 | bytes 14680064 | tf_op jit(solution)/shard_map/bj,ij->bi/dot_general | solution.py:229
  48.7 2.1 copy-done.42
  50.8 6.5 %fusion.99 = f32[1024,1024]{1,0:T(8,128)} fusion(bf16[2048,1024]{1,0:T(8,128)(2,1)S(1)} %fusion.15), kind=kOutput, calls=%fused_computation.205 | convolution fusion | flops 4294967296 | bytes 8388608 | tf_op jit(solution)/shard_map/bi,bj->ij/dot_general | solution.py:23
  57.3 3.3 dynamic-slice_bitcast_fusion.3
  61.4 6.4 %fusion.97 = f32[1024,1024]{0,1:T(8,128)S(1)} fusion(bf16[2048,1024]{1,0:T(8,128)(2,1)} %copy-done.42, bf16[2048,1024]{1,0:T(8,128)(2,1)S(1)} %copy-done.35), kind=kOutput, calls=%fused_computation.203 | convolution fusion | flops 4294967296 | bytes 12582912 | tf_op jit(solution)/shard_map/bi,bj->ij/dot_general | solution.py:23
  69.4 2.8 copy-done.41
  72.2 4.8 fusion.101
  77.0 2.1 copy-done.3
  81.4 6.1 %fusion.94 = f32[1024,1024]{1,0:T(8,128)S(1)} fusion(bf16[2048,1024]{1,0:T(8,128)(2,1)S(1)} %copy-done.41, bf16[2048,1024]{1,0:T(8,128)(2,1)S(1)} %copy-done.48), kind=kOutput, calls=%fused_computation.202 | convolution fusion | flops 4315938816 | bytes 12582912 | tf_op jit(solution)/shard_map/bi,bj->ij/dot_general | solution.py:23
  90.1 8.0 %fusion.92 = f32[1024,1024]{1,0:T(8,128)S(1)} fusion(bf16[2048,1024]{1,0:T(8,128)(2,1)S(1)} %copy-done.48), kind=kOutput, calls=%fused_computation.201 | convolution fusion | flops 4315938816 | bytes 8388608 | tf_op jit(solution)/shard_map/bi,bj->ij/dot_general | solution.py:23
  100.2 2.3 copy-done.39
  102.5 4.7 fusion.100
  107.3 6.3 %fusion.89 = f32[1024,1024]{1,0:T(8,128)S(1)} fusion(bf16[2048,1024]{1,0:T(8,128)(2,1)S(1)} %copy-done.39, bf16[2048,1024]{1,0:T(8,128)(2,1)S(1)} %copy-done.46), kind=kOutput, calls=%fused_computation.200 | convolution fusion | flops 4315938816 | bytes 12582912 | tf_op jit(solution)/shard_map/bi,bj->ij/dot_general | solution.py:23
  113.6 13.0 %fusion.87 = f32[1024,1024]{1,0:T(8,128)S(1)} fusion(bf16[2048,1024]{1,0:T(8,128)(2,1)} %copy-done.45), kind=kOutput, calls=%fused_computation.199 | convolution fusion | flops 4315938816 | bytes 8388608 | tf_op jit(solution)/shard_map/bi,bj->ij/dot_general | solution.py:23
  126.6 8.2 %fusion.83 = f32[1024,1024]{1,0:T(8,128)S(1)} fusion(bf16[2048,1024]{1,0:T(8,128)(2,1)S(1)} %copy-done.44), kind=kOutput, calls=%fused_computation.197 | convolution fusion | flops 4315938816 | bytes 8388608 | tf_op jit(solution)/shard_map/bi,bj->ij/dot_general | solution.py:23
  134.8 9.1 %fusion.98 = f32[1024,1024]{1,0:T(8,128)S(1)} fusion(bf16[2048,1024]{1,0:T(8,128)(2,1)} %param.7), kind=kOutput, calls=%fused_computation.204 | convolution fusion | flops 4294967296 | bytes 8388608 | tf_op jit(solution)/shard_map/bi,bj->ij/dot_general | solution.py:23
  143.9 9.1 %fusion.102 = f32[1024,1024]{1,0:T(8,128)S(1)} fusion(bf16[2048,1024]{1,0:T(8,128)(2,1)} %param.8), kind=kOutput, calls=%fused_computation.208 | convolution fusion | flops 4294967296 | bytes 8388608 | tf_op jit(solution)/shard_map/bi,bj->ij/dot_general | solution.py:23
  158.5 2.1 copy-done.37
  160.6 6.7 %fusion.85 = f32[1024,1024]{1,0:T(8,128)S(1)} fusion(bf16[2048,1024]{1,0:T(8,128)(2,1)S(1)} %copy-done.37, bf16[2048,1024]{1,0:T(8,128)(2,1)} %copy-done.43), kind=kOutput, calls=%fused_computation.198 | convolution fusion | flops 4315938816 | bytes 12582912 | tf_op jit(solution)/shard_map/bi,bj->ij/dot_general | solution.py:23
  177.5 2.3 fusion.57
  181.5 2.3 fusion.53
  185.6 2.7 fusion.61
  189.2 2.1 fusion.71
  191.3 2.8 collective-permute-start.1
  194.1 2.1 fusion.63
  196.4 2.3 fusion.59
  202.7 2.3 fusion.65
  206.4 2.1 fusion.51
  210.7 18.6 %collective-permute-done.5 = bf16[256,1024]{1,0:T(8,128)(2,1)S(1)} collective-permute-done((bf16[256,1024]{1,0:T(8,128)(2,1)S(1)}, bf16[256,1024]{1,0:T(8,128)(2,1)S(1)}, u32[]{:S(2)}, u32[]{:S(2)}) %collective-permute-start.5) | collective-permute-done | bytes 524320 | tf_op jit(solution)/shard_map/ppermute | solution.py:187
  232.8 30.2 %collective-permute-done.3 = bf16[256,1024]{1,0:T(8,128)(2,1)S(1)} collective-permute-done((bf16[256,1024]{1,0:T(8,128)(2,1)S(1)}, bf16[256,1024]{1,0:T(8,128)(2,1)S(1)}, u32[]{:S(2)}, u32[]{:S(2)}) %collective-permute-start.3) | collective-permute-done | bytes 524320 | tf_op jit(solution)/shard_map/ppermute | solution.py:187
  266.5 7.7 %collective-permute-done.7 = bf16[256,1024]{1,0:T(8,128)(2,1)S(1)} collective-permute-done((bf16[256,1024]{1,0:T(8,128)(2,1)S(1)}, bf16[256,1024]{1,0:T(8,128)(2,1)S(1)}, u32[]{:S(2)}, u32[]{:S(2)}) %collective-permute-start.7) | collective-permute-done | bytes 524320 | tf_op jit(solution)/shard_map/ppermute | solution.py:187
  282.5 14.2 %collective-permute-done.15 = bf16[256,1024]{1,0:T(8,128)(2,1)} collective-permute-done((bf16[256,1024]{1,0:T(8,128)(2,1)}, bf16[256,1024]{1,0:T(8,128)(2,1)}, u32[]{:S(2)}, u32[]{:S(2)}) %collective-permute-start.15) | collective-permute-done | bytes 524320 | tf_op jit(solution)/shard_map/ppermute | solution.py:187
  300.4 7.6 %collective-permute-done.19 = bf16[256,1024]{1,0:T(8,128)(2,1)S(1)} collective-permute-done((bf16[256,1024]{1,0:T(8,128)(2,1)}, bf16[256,1024]{1,0:T(8,128)(2,1)S(1)}, u32[]{:S(2)}, u32[]{:S(2)}) %collective-permute-start.19) | collective-permute-done | bytes 524320 | tf_op jit(solution)/shard_map/ppermute | solution.py:187
  311.5 7.7 %collective-permute-done.13 = bf16[256,1024]{1,0:T(8,128)(2,1)S(1)} collective-permute-done((bf16[256,1024]{1,0:T(8,128)(2,1)S(1)}, bf16[256,1024]{1,0:T(8,128)(2,1)S(1)}, u32[]{:S(2)}, u32[]{:S(2)}) %collective-permute-start.13) | collective-permute-done | bytes 524320 | tf_op jit(solution)/shard_map/ppermute | solution.py:187
  334.4 22.1 %collective-permute-done.22 = bf16[2,256,512]{2,1,0:T(8,128)(2,1)S(1)} collective-permute-done((bf16[2,256,512]{2,1,0:T(8,128)(2,1)S(1)}, bf16[2,256,512]{2,1,0:T(8,128)(2,1)S(1)}, u32[]{:S(2)}, u32[]{:S(2)}) %collective-permute-start.22) | collective-permute-done | bytes 524320 | tf_op jit(solution)/shard_map/ppermute | solution.py:187
  356.5 2.1 collective-permute-start.32
  362.3 3.7 collective-permute-done.34
  367.8 3.6 collective-permute-done.32
  376.3 6.3 %collective-permute-done.23 = f32[256,512]{1,0:T(8,128)S(1)} collective-permute-done((f32[256,512]{1,0:T(8,128)S(1)}, f32[256,512]{1,0:T(8,128)S(1)}, u32[]{:S(2)}, u32[]{:S(2)}) %collective-permute-start.23) | collective-permute-done | bytes 524320 | tf_op jit(solution)/shard_map/ppermute | solution.py:187
  384.9 8.9 %collective-permute-done.35 = f32[256,512]{1,0:T(8,128)S(1)} collective-permute-done((f32[256,512]{1,0:T(8,128)S(1)}, f32[256,512]{1,0:T(8,128)S(1)}, u32[]{:S(2)}, u32[]{:S(2)}) %collective-permute-start.35) | collective-permute-done | bytes 524320 | tf_op jit(solution)/shard_map/ppermute | solution.py:187
  396.7 6.2 %collective-permute-done.11 = f32[256,512]{1,0:T(8,128)S(1)} collective-permute-done((f32[256,512]{1,0:T(8,128)S(1)}, f32[256,512]{1,0:T(8,128)S(1)}, u32[]{:S(2)}, u32[]{:S(2)}) %collective-permute-start.11) | collective-permute-done | bytes 524320 | tf_op jit(solution)/shard_map/ppermute | solution.py:187
  403.3 72.1 %shard_map.94 = bf16[16,272,1024]{2,1,0:T(8,128)(2,1)} custom-call(f32[256,1024]{1,0:T(8,128)S(1)} %maximum_multiply_fusion.g_ref, f32[256,1024]{1,0:T(8,128)S(1)} %copy-done, f32[4,1024,1024]{2,1,0:T(8,128)} %sinv_hbm.1), custom_call_target="tpu_custom_call" | custom-call | flops 6442450944 | bytes 20971520 | tf_op jit(solution)/shard_map/pallas_call | solution.py:155
  476.4 13.1 %select_select_fusion = f32[16,256,1024]{2,1,0:T(8,128)} fusion(f32[16]{0:T(128)S(1)} %multiply_reduce_fusion, bf16[16,272,1024]{2,1,0:T(8,128)(2,1)} %shard_map.94), kind=kLoop, calls=%fused_computation.8 | loop fusion | flops 46137344 | bytes 25165888 | tf_op jit(solution)/shard_map/jit(_where)/select_n | solution.py:36
  (211 shorter events, 91.3 us)
Async XLA Ops:
  8.2 30.8 %copy-start.47 = (bf16[2048,1024]{1,0:T(8,128)(2,1)}, bf16[2048,1024]{1,0:T(8,128)(2,1)S(1)}, u32[]{:S(2)}) copy-start(bf16[2048,1024]{1,0:T(8,128)(2,1)S(1)} %convolution_convert_fusion.2) | copy-start | bytes 12582916
  60.6 94.2 %collective-permute-start.24 = (f32[2,256,1024]{2,1,0:T(8,128)}, f32[2,256,1024]{2,1,0:T(8,128)S(1)}, u32[]{:S(2)}, u32[]{:S(2)}) collective-permute-start(f32[2,256,1024]{2,1,0:T(8,128)} %dynamic-slice_bitcast_fusion.3), channel_id=1, source_target_pairs={{0,1},{1,0},{2,3},{3,2},{4,5},{5,4},{6,7},{7,6},{8,9},{9,8},{10,11... | collective-permute-start | bytes 6291464 | tf_op jit(solution)/shard_map/ppermute | solution.py:187
  69.4 87.5 %collective-permute-start = (f32[2,256,1024]{2,1,0:T(8,128)}, f32[2,256,1024]{2,1,0:T(8,128)S(1)}, u32[]{:S(2)}, u32[]{:S(2)}) collective-permute-start(f32[2,256,1024]{2,1,0:T(8,128)} %dynamic-slice_bitcast_fusion.11), channel_id=1, source_target_pairs={{0,1},{1,0},{2,3},{3,2},{4,5},{5,4},{6,7},{7,6},{8,9},{9,8},{10,11... | collective-permute-start | bytes 6291464 | tf_op jit(solution)/shard_map/ppermute | solution.py:187
  80.7 86.7 %collective-permute-start.28 = (f32[2,256,1024]{2,1,0:T(8,128)}, f32[2,256,1024]{2,1,0:T(8,128)S(1)}, u32[]{:S(2)}, u32[]{:S(2)}) collective-permute-start(f32[2,256,1024]{2,1,0:T(8,128)} %dynamic-slice_bitcast_fusion.1), channel_id=1, source_target_pairs={{0,1},{1,0},{2,3},{3,2},{4,5},{5,4},{6,7},{7,6},{8,9},{9,8},{10,11... | collective-permute-start | bytes 6291464 | tf_op jit(solution)/shard_map/ppermute | solution.py:187
  90.1 79.2 %collective-permute-start.4 = (f32[2,256,1024]{2,1,0:T(8,128)}, f32[2,256,1024]{2,1,0:T(8,128)S(1)}, u32[]{:S(2)}, u32[]{:S(2)}) collective-permute-start(f32[2,256,1024]{2,1,0:T(8,128)} %dynamic-slice_bitcast_fusion.9), channel_id=1, source_target_pairs={{0,1},{1,0},{2,3},{3,2},{4,5},{5,4},{6,7},{7,6},{8,9},{9,8},{10,11... | collective-permute-start | bytes 6291464 | tf_op jit(solution)/shard_map/ppermute | solution.py:187
  99.7 72.2 %collective-permute-start.16 = (f32[2,256,1024]{2,1,0:T(8,128)}, f32[2,256,1024]{2,1,0:T(8,128)S(1)}, u32[]{:S(2)}, u32[]{:S(2)}) collective-permute-start(f32[2,256,1024]{2,1,0:T(8,128)} %dynamic-slice_bitcast_fusion.5), channel_id=1, source_target_pairs={{0,1},{1,0},{2,3},{3,2},{4,5},{5,4},{6,7},{7,6},{8,9},{9,8},{10,11... | collective-permute-start | bytes 6291464 | tf_op jit(solution)/shard_map/ppermute | solution.py:187
  107.3 45.8 %copy-start.5 = (f32[1024,1024]{1,0:T(8,128)}, f32[1024,1024]{1,0:T(8,128)S(1)}, u32[]{:S(2)}) copy-start(f32[1024,1024]{1,0:T(8,128)S(1)} %fusion.100) | copy-start | bytes 12582916
  113.6 41.7 %copy-start.16 = (f32[1024,1024]{1,0:T(8,128)}, f32[1024,1024]{1,0:T(8,128)S(1)}, u32[]{:S(2)}) copy-start(f32[1024,1024]{1,0:T(8,128)S(1)} %fusion.89) | copy-start | bytes 12582916
  126.6 30.3 %copy-start.11 = (f32[1024,1024]{1,0:T(8,128)}, f32[1024,1024]{1,0:T(8,128)S(1)}, u32[]{:S(2)}) copy-start(f32[1024,1024]{1,0:T(8,128)S(1)} %fusion.87) | copy-start | bytes 12582916
  134.8 32.7 %copy-start.9 = (f32[1024,1024]{1,0:T(8,128)}, f32[1024,1024]{1,0:T(8,128)S(1)}, u32[]{:S(2)}) copy-start(f32[1024,1024]{1,0:T(8,128)S(1)} %fusion.83) | copy-start | bytes 12582916
  143.9 28.1 %copy-start.7 = (f32[1024,1024]{1,0:T(8,128)}, f32[1024,1024]{1,0:T(8,128)S(1)}, u32[]{:S(2)}) copy-start(f32[1024,1024]{1,0:T(8,128)S(1)} %fusion.98) | copy-start | bytes 12582916
  153.0 21.1 %copy-start.1 = (f32[1024,1024]{1,0:T(8,128)}, f32[1024,1024]{1,0:T(8,128)S(1)}, u32[]{:S(2)}) copy-start(f32[1024,1024]{1,0:T(8,128)S(1)} %fusion.102) | copy-start | bytes 12582916
  154.8 19.0 %collective-permute-start.26 = (f32[2,256,1024]{2,1,0:T(8,128)}, f32[2,256,1024]{2,1,0:T(8,128)S(1)}, u32[]{:S(2)}, u32[]{:S(2)}) collective-permute-start(f32[2,256,1024]{2,1,0:T(8,128)} %dynamic-slice_bitcast_fusion.2), channel_id=1, source_target_pairs={{0,1},{1,0},{2,3},{3,2},{4,5},{5,4},{6,7},{7,6},{8,9},{9,8},{10,11... | collective-permute-start | bytes 6291464 | tf_op jit(solution)/shard_map/ppermute | solution.py:187
  156.9 19.0 %collective-permute-start.2 = (f32[2,256,1024]{2,1,0:T(8,128)}, f32[2,256,1024]{2,1,0:T(8,128)S(1)}, u32[]{:S(2)}, u32[]{:S(2)}) collective-permute-start(f32[2,256,1024]{2,1,0:T(8,128)} %dynamic-slice_bitcast_fusion.10), channel_id=1, source_target_pairs={{0,1},{1,0},{2,3},{3,2},{4,5},{5,4},{6,7},{7,6},{8,9},{9,8},{10,11... | collective-permute-start | bytes 6291464 | tf_op jit(solution)/shard_map/ppermute | solution.py:187
  167.4 23.9 %collective-permute-start.14 = (f32[2,256,1024]{2,1,0:T(8,128)}, f32[2,256,1024]{2,1,0:T(8,128)}, u32[]{:S(2)}, u32[]{:S(2)}) collective-permute-start(f32[2,256,1024]{2,1,0:T(8,128)} %dynamic-slice_bitcast_fusion.6), channel_id=1, source_target_pairs={{0,1},{1,0},{2,3},{3,2},{4,5},{5,4},{6,7},{7,6},{8,9},{9,8},{10,11... | collective-permute-start | bytes 6291464 | tf_op jit(solution)/shard_map/ppermute | solution.py:187
  169.3 26.9 %collective-permute-start.18 = (f32[2,256,1024]{2,1,0:T(8,128)}, f32[2,256,1024]{2,1,0:T(8,128)}, u32[]{:S(2)}, u32[]{:S(2)}) collective-permute-start(f32[2,256,1024]{2,1,0:T(8,128)} %dynamic-slice_bitcast_fusion.4), channel_id=1, source_target_pairs={{0,1},{1,0},{2,3},{3,2},{4,5},{5,4},{6,7},{7,6},{8,9},{9,8},{10,11... | collective-permute-start | bytes 6291464 | tf_op jit(solution)/shard_map/ppermute | solution.py:187
  171.9 26.8 %collective-permute-start.6 = (f32[2,256,1024]{2,1,0:T(8,128)}, f32[2,256,1024]{2,1,0:T(8,128)}, u32[]{:S(2)}, u32[]{:S(2)}) collective-permute-start(f32[2,256,1024]{2,1,0:T(8,128)} %dynamic-slice_bitcast_fusion.8), channel_id=1, source_target_pairs={{0,1},{1,0},{2,3},{3,2},{4,5},{5,4},{6,7},{7,6},{8,9},{9,8},{10,11... | collective-permute-start | bytes 6291464 | tf_op jit(solution)/shard_map/ppermute | solution.py:187
  173.8 28.3 %collective-permute-start.12 = (f32[2,256,1024]{2,1,0:T(8,128)}, f32[2,256,1024]{2,1,0:T(8,128)}, u32[]{:S(2)}, u32[]{:S(2)}) collective-permute-start(f32[2,256,1024]{2,1,0:T(8,128)} %dynamic-slice_bitcast_fusion.7), channel_id=1, source_target_pairs={{0,1},{1,0},{2,3},{3,2},{4,5},{5,4},{6,7},{7,6},{8,9},{9,8},{10,11... | collective-permute-start | bytes 6291464 | tf_op jit(solution)/shard_map/ppermute | solution.py:187
  177.2 27.7 %collective-permute-start.30 = (f32[2,256,1024]{2,1,0:T(8,128)}, f32[2,256,1024]{2,1,0:T(8,128)}, u32[]{:S(2)}, u32[]{:S(2)}) collective-permute-start(f32[2,256,1024]{2,1,0:T(8,128)} %dynamic-slice_bitcast_fusion), channel_id=1, source_target_pairs={{0,1},{1,0},{2,3},{3,2},{4,5},{5,4},{6,7},{7,6},{8,9},{9,8},{10,11... | collective-permute-start | bytes 6291464 | tf_op jit(solution)/shard_map/ppermute | solution.py:187
  191.3 17.2 %collective-permute-start.1 = (bf16[256,1024]{1,0:T(8,128)(2,1)S(1)}, bf16[256,1024]{1,0:T(8,128)(2,1)S(1)}, u32[]{:S(2)}, u32[]{:S(2)}) collective-permute-start(bf16[256,1024]{1,0:T(8,128)(2,1)S(1)} %fusion.73), channel_id=1, source_target_pairs={{0,2},{1,3},{2,0},{3,1},{4,6},{5,7},{6,4},{7,5},{8,10},{9,11},{10,... | collective-permute-start | bytes 1572872 | tf_op jit(solution)/shard_map/ppermute | solution.py:187
  196.2 126.9 %collective-permute-start.25 = (bf16[256,1024]{1,0:T(8,128)(2,1)}, bf16[256,1024]{1,0:T(8,128)(2,1)}, u32[]{:S(2)}, u32[]{:S(2)}) collective-permute-start(bf16[256,1024]{1,0:T(8,128)(2,1)} %fusion.57), channel_id=1, source_target_pairs={{0,2},{1,3},{2,0},{3,1},{4,6},{5,7},{6,4},{7,5},{8,10},{9,11},{10,... | collective-permute-start | bytes 1572872 | tf_op jit(solution)/shard_map/ppermute | solution.py:187
  198.7 30.6 %collective-permute-start.5 = (bf16[256,1024]{1,0:T(8,128)(2,1)S(1)}, bf16[256,1024]{1,0:T(8,128)(2,1)S(1)}, u32[]{:S(2)}, u32[]{:S(2)}) collective-permute-start(bf16[256,1024]{1,0:T(8,128)(2,1)S(1)} %fusion.69), channel_id=1, source_target_pairs={{0,2},{1,3},{2,0},{3,1},{4,6},{5,7},{6,4},{7,5},{8,10},{9,11},{10,... | collective-permute-start | bytes 1572872 | tf_op jit(solution)/shard_map/ppermute | solution.py:187
  202.1 29.2 %copy-start.27 = (f32[2,256,1024]{2,1,0:T(8,128)S(1)}, f32[2,256,1024]{2,1,0:T(8,128)}, u32[]{:S(2)}) copy-start(f32[2,256,1024]{2,1,0:T(8,128)} %copy-done.26) | copy-start | bytes 6291460
  202.1 124.3 %collective-permute-start.29 = (bf16[256,1024]{1,0:T(8,128)(2,1)}, bf16[256,1024]{1,0:T(8,128)(2,1)}, u32[]{:S(2)}, u32[]{:S(2)}) collective-permute-start(bf16[256,1024]{1,0:T(8,128)(2,1)} %fusion.53), channel_id=1, source_target_pairs={{0,2},{1,3},{2,0},{3,1},{4,6},{5,7},{6,4},{7,5},{8,10},{9,11},{10,... | collective-permute-start | bytes 1572872 | tf_op jit(solution)/shard_map/ppermute | solution.py:187
  204.9 75.8 %collective-permute-start.17 = (bf16[256,1024]{1,0:T(8,128)(2,1)}, bf16[256,1024]{1,0:T(8,128)(2,1)}, u32[]{:S(2)}, u32[]{:S(2)}) collective-permute-start(bf16[256,1024]{1,0:T(8,128)(2,1)} %fusion.61), channel_id=1, source_target_pairs={{0,2},{1,3},{2,0},{3,1},{4,6},{5,7},{6,4},{7,5},{8,10},{9,11},{10,... | collective-permute-start | bytes 1572872 | tf_op jit(solution)/shard_map/ppermute | solution.py:187
  208.6 56.5 %copy-start.29 = (f32[2,256,1024]{2,1,0:T(8,128)S(1)}, f32[2,256,1024]{2,1,0:T(8,128)}, u32[]{:S(2)}) copy-start(f32[2,256,1024]{2,1,0:T(8,128)} %copy-done.28) | copy-start | bytes 6291460
  208.6 54.5 %collective-permute-start.3 = (bf16[256,1024]{1,0:T(8,128)(2,1)S(1)}, bf16[256,1024]{1,0:T(8,128)(2,1)S(1)}, u32[]{:S(2)}, u32[]{:S(2)}) collective-permute-start(bf16[256,1024]{1,0:T(8,128)(2,1)S(1)} %fusion.71), channel_id=1, source_target_pairs={{0,2},{1,3},{2,0},{3,1},{4,6},{5,7},{6,4},{7,5},{8,10},{9,11},{10,... | collective-permute-start | bytes 1572872 | tf_op jit(solution)/shard_map/ppermute | solution.py:187
  229.3 44.9 %collective-permute-start.7 = (bf16[256,1024]{1,0:T(8,128)(2,1)S(1)}, bf16[256,1024]{1,0:T(8,128)(2,1)S(1)}, u32[]{:S(2)}, u32[]{:S(2)}) collective-permute-start(bf16[256,1024]{1,0:T(8,128)(2,1)S(1)} %fusion.67), channel_id=1, source_target_pairs={{0,2},{1,3},{2,0},{3,1},{4,6},{5,7},{6,4},{7,5},{8,10},{9,11},{10,... | collective-permute-start | bytes 1572872 | tf_op jit(solution)/shard_map/ppermute | solution.py:187
  263.0 65.2 %collective-permute-start.27 = (bf16[256,1024]{1,0:T(8,128)(2,1)}, bf16[256,1024]{1,0:T(8,128)(2,1)}, u32[]{:S(2)}, u32[]{:S(2)}) collective-permute-start(bf16[256,1024]{1,0:T(8,128)(2,1)} %fusion.55), channel_id=1, source_target_pairs={{0,2},{1,3},{2,0},{3,1},{4,6},{5,7},{6,4},{7,5},{8,10},{9,11},{10,... | collective-permute-start | bytes 1572872 | tf_op jit(solution)/shard_map/ppermute | solution.py:187
  274.3 22.5 %collective-permute-start.15 = (bf16[256,1024]{1,0:T(8,128)(2,1)}, bf16[256,1024]{1,0:T(8,128)(2,1)}, u32[]{:S(2)}, u32[]{:S(2)}) collective-permute-start(bf16[256,1024]{1,0:T(8,128)(2,1)} %fusion.63), channel_id=1, source_target_pairs={{0,2},{1,3},{2,0},{3,1},{4,6},{5,7},{6,4},{7,5},{8,10},{9,11},{10,... | collective-permute-start | bytes 1572872 | tf_op jit(solution)/shard_map/ppermute | solution.py:187
  279.6 17.1 %copy-start.33 = (bf16[256,1024]{1,0:T(8,128)(2,1)S(1)}, bf16[256,1024]{1,0:T(8,128)(2,1)}, u32[]{:S(2)}) copy-start(bf16[256,1024]{1,0:T(8,128)(2,1)} %fusion.65) | copy-start | bytes 1572868
  280.8 27.2 %copy-start.32 = (bf16[256,1024]{1,0:T(8,128)(2,1)S(1)}, bf16[256,1024]{1,0:T(8,128)(2,1)}, u32[]{:S(2)}) copy-start(bf16[256,1024]{1,0:T(8,128)(2,1)} %fusion.51) | copy-start | bytes 1572868
  280.8 27.2 %collective-permute-start.19 = (bf16[256,1024]{1,0:T(8,128)(2,1)}, bf16[256,1024]{1,0:T(8,128)(2,1)S(1)}, u32[]{:S(2)}, u32[]{:S(2)}) collective-permute-start(bf16[256,1024]{1,0:T(8,128)(2,1)} %fusion.59), channel_id=1, source_target_pairs={{0,2},{1,3},{2,0},{3,1},{4,6},{5,7},{6,4},{7,5},{8,10},{9,11},{10,... | collective-permute-start | bytes 1572872 | tf_op jit(solution)/shard_map/ppermute | solution.py:187
  296.7 22.5 %collective-permute-start.13 = (bf16[256,1024]{1,0:T(8,128)(2,1)S(1)}, bf16[256,1024]{1,0:T(8,128)(2,1)S(1)}, u32[]{:S(2)}, u32[]{:S(2)}) collective-permute-start(bf16[256,1024]{1,0:T(8,128)(2,1)S(1)} %copy-done.33), channel_id=1, source_target_pairs={{0,2},{1,3},{2,0},{3,1},{4,6},{5,7},{6,4},{7,5},{8,10},{9,11},{10,... | collective-permute-start | bytes 1572872 | tf_op jit(solution)/shard_map/ppermute | solution.py:187
  308.0 22.3 %collective-permute-start.31 = (bf16[256,1024]{1,0:T(8,128)(2,1)S(1)}, bf16[256,1024]{1,0:T(8,128)(2,1)S(1)}, u32[]{:S(2)}, u32[]{:S(2)}) collective-permute-start(bf16[256,1024]{1,0:T(8,128)(2,1)S(1)} %copy-done.32), channel_id=1, source_target_pairs={{0,2},{1,3},{2,0},{3,1},{4,6},{5,7},{6,4},{7,5},{8,10},{9,11},{10,... | collective-permute-start | bytes 1572872 | tf_op jit(solution)/shard_map/ppermute | solution.py:187
  319.2 54.4 %collective-permute-start.10 = (f32[2,256,512]{2,1,0:T(8,128)S(1)}, f32[2,256,512]{2,1,0:T(8,128)S(1)}, u32[]{:S(2)}, u32[]{:S(2)}) collective-permute-start(f32[2,256,512]{2,1,0:T(8,128)S(1)} %pad_maximum_fusion.1), channel_id=1, source_target_pairs={{0,4},{1,5},{2,6},{3,7},{4,0},{5,1},{6,2},{7,3},{8,12},{9,13},{10,... | collective-permute-start | bytes 3145736 | tf_op jit(solution)/shard_map/ppermute | solution.py:187
  323.1 52.4 %collective-permute-start.8 = (f32[2,256,512]{2,1,0:T(8,128)S(1)}, f32[2,256,512]{2,1,0:T(8,128)S(1)}, u32[]{:S(2)}, u32[]{:S(2)}) collective-permute-start(f32[2,256,512]{2,1,0:T(8,128)S(1)} %pad_maximum_fusion), channel_id=1, source_target_pairs={{0,8},{1,9},{2,10},{3,11},{4,12},{5,13},{6,14},{7,15},{8,0},{9,1},... | collective-permute-start | bytes 3145736 | tf_op jit(solution)/shard_map/ppermute | solution.py:187
  326.4 30.1 %collective-permute-start.22 = (bf16[2,256,512]{2,1,0:T(8,128)(2,1)S(1)}, bf16[2,256,512]{2,1,0:T(8,128)(2,1)S(1)}, u32[]{:S(2)}, u32[]{:S(2)}) collective-permute-start(bf16[2,256,512]{2,1,0:T(8,128)(2,1)S(1)} %pad_maximum_fusion.3), channel_id=1, source_target_pairs={{0,4},{1,5},{2,6},{3,7},{4,0},{5,1},{6,2},{7,3},{8,12},{9,13},{10,... | collective-permute-start | bytes 1572872 | tf_op jit(solution)/shard_map/ppermute | solution.py:187
  328.3 31.8 %collective-permute-start.20 = (bf16[2,256,512]{2,1,0:T(8,128)(2,1)S(1)}, bf16[2,256,512]{2,1,0:T(8,128)(2,1)S(1)}, u32[]{:S(2)}, u32[]{:S(2)}) collective-permute-start(bf16[2,256,512]{2,1,0:T(8,128)(2,1)S(1)} %pad_maximum_fusion.2), channel_id=1, source_target_pairs={{0,8},{1,9},{2,10},{3,11},{4,12},{5,13},{6,14},{7,15},{8,0},{9,1},... | collective-permute-start | bytes 1572872 | tf_op jit(solution)/shard_map/ppermute | solution.py:187
  332.0 34.0 %collective-permute-start.34 = (bf16[2,256,512]{2,1,0:T(8,128)(2,1)S(1)}, bf16[2,256,512]{2,1,0:T(8,128)(2,1)S(1)}, u32[]{:S(2)}, u32[]{:S(2)}) collective-permute-start(bf16[2,256,512]{2,1,0:T(8,128)(2,1)S(1)} %pad_maximum_fusion.5), channel_id=1, source_target_pairs={{0,4},{1,5},{2,6},{3,7},{4,0},{5,1},{6,2},{7,3},{8,12},{9,13},{10,... | collective-permute-start | bytes 1572872 | tf_op jit(solution)/shard_map/ppermute | solution.py:187
  356.5 14.9 %collective-permute-start.32 = (bf16[2,256,512]{2,1,0:T(8,128)(2,1)S(1)}, bf16[2,256,512]{2,1,0:T(8,128)(2,1)S(1)}, u32[]{:S(2)}, u32[]{:S(2)}) collective-permute-start(bf16[2,256,512]{2,1,0:T(8,128)(2,1)S(1)} %pad_maximum_fusion.4), channel_id=1, source_target_pairs={{0,8},{1,9},{2,10},{3,11},{4,12},{5,13},{6,14},{7,15},{8,0},{9,1},... | collective-permute-start | bytes 1572872 | tf_op jit(solution)/shard_map/ppermute | solution.py:187
  360.1 22.5 %collective-permute-start.23 = (f32[256,512]{1,0:T(8,128)S(1)}, f32[256,512]{1,0:T(8,128)S(1)}, u32[]{:S(2)}, u32[]{:S(2)}) collective-permute-start(f32[256,512]{1,0:T(8,128)S(1)} %select_bitcast_fusion.6), channel_id=1, source_target_pairs={{0,8},{1,9},{2,10},{3,11},{4,12},{5,13},{6,14},{7,15},{8,0},{9,1},... | collective-permute-start | bytes 1572872 | tf_op jit(solution)/shard_map/ppermute | solution.py:187
  366.0 18.7 %collective-permute-start.21 = (f32[256,512]{1,0:T(8,128)S(1)}, f32[256,512]{1,0:T(8,128)S(1)}, u32[]{:S(2)}, u32[]{:S(2)}) collective-permute-start(f32[256,512]{1,0:T(8,128)S(1)} %select_bitcast_fusion.9), channel_id=1, source_target_pairs={{0,4},{1,5},{2,6},{3,7},{4,0},{5,1},{6,2},{7,3},{8,12},{9,13},{10,... | collective-permute-start | bytes 1572872 | tf_op jit(solution)/shard_map/ppermute | solution.py:187
  371.4 22.5 %collective-permute-start.35 = (f32[256,512]{1,0:T(8,128)S(1)}, f32[256,512]{1,0:T(8,128)S(1)}, u32[]{:S(2)}, u32[]{:S(2)}) collective-permute-start(f32[256,512]{1,0:T(8,128)S(1)} %select_bitcast_fusion), channel_id=1, source_target_pairs={{0,8},{1,9},{2,10},{3,11},{4,12},{5,13},{6,14},{7,15},{8,0},{9,1},... | collective-permute-start | bytes 1572872 | tf_op jit(solution)/shard_map/ppermute | solution.py:187
  373.7 21.5 %collective-permute-start.33 = (f32[256,512]{1,0:T(8,128)S(1)}, f32[256,512]{1,0:T(8,128)S(1)}, u32[]{:S(2)}, u32[]{:S(2)}) collective-permute-start(f32[256,512]{1,0:T(8,128)S(1)} %select_bitcast_fusion.3), channel_id=1, source_target_pairs={{0,4},{1,5},{2,6},{3,7},{4,0},{5,1},{6,2},{7,3},{8,12},{9,13},{10,... | collective-permute-start | bytes 1572872 | tf_op jit(solution)/shard_map/ppermute | solution.py:187
  375.5 27.3 %collective-permute-start.11 = (f32[256,512]{1,0:T(8,128)S(1)}, f32[256,512]{1,0:T(8,128)S(1)}, u32[]{:S(2)}, u32[]{:S(2)}) collective-permute-start(f32[256,512]{1,0:T(8,128)S(1)} %select_bitcast_fusion.12), channel_id=1, source_target_pairs={{0,8},{1,9},{2,10},{3,11},{4,12},{5,13},{6,14},{7,15},{8,0},{9,1},... | collective-permute-start | bytes 1572872 | tf_op jit(solution)/shard_map/ppermute | solution.py:187
  376.2 17.8 %copy-start.30 = (f32[256,1024]{1,0:T(8,128)S(1)}, f32[256,1024]{1,0:T(8,128)}, u32[]{:S(2)}) copy-start(f32[256,1024]{1,0:T(8,128)} %param.10) | copy-start | bytes 3145732
  382.6 20.4 %collective-permute-start.9 = (f32[256,512]{1,0:T(8,128)S(1)}, f32[256,512]{1,0:T(8,128)S(1)}, u32[]{:S(2)}, u32[]{:S(2)}) collective-permute-start(f32[256,512]{1,0:T(8,128)S(1)} %select_bitcast_fusion.17), channel_id=1, source_target_pairs={{0,4},{1,5},{2,6},{3,7},{4,0},{5,1},{6,2},{7,3},{8,12},{9,13},{10,... | collective-permute-start | bytes 1572872 | tf_op jit(solution)/shard_map/ppermute | solution.py:187
  (37 other events, 246.9 us)
